TPU v7x, 32 devices: a whole 2x2x4 slice. The times are simulated.
32 devices in a mesh: dp: 8 (over z, y), tensor: 4 (over x, core).
Axes of the slice: x: 2, y: 2, z: 4, core: 2. Of those that a mesh axis runs over, the one named last changes fastest.
Arguments:
- image_rows: bfloat16 [16, 197, 768], P('dp', None, 'tensor'), may hold values from -6 to 6
- text_rows: bfloat16 [8, 512, 768], P('dp', None, 'tensor'), may hold values from -6 to 6
- pair_rows: bfloat16 [8, 711, 768], P('dp', None, 'tensor'), may hold values from -6 to 6
- text_lengths: int32 [8], P('dp'), may hold values from 128 to 512, as said below
- pair_lengths: int32 [8], P('dp'), may hold values from 128 to 512, as said below
- qkv_weight: bfloat16 [3, 768, 3, 768], P(None, None, None, 'tensor'), may hold values from -0.21875 to 0.21875
- qv_bias: bfloat16 [3, 2, 768], P(None, None, 'tensor'), may hold values from -3 to 3
- out_weight: bfloat16 [3, 768, 768], P(None, 'tensor'), may hold values from -3.5 to 3.5
- out_bias: bfloat16 [3, 768], P(None, 'tensor'), may hold values from -3 to 3
- up_weight: bfloat16 [3, 768, 3072], P(None, None, 'tensor'), may hold values from -0.21875 to 0.21875
- up_bias: bfloat16 [3, 3072], P(None, 'tensor'), may hold values from -3 to 3
- down_weight: bfloat16 [3, 3072, 768], P(None, 'tensor'), may hold values from -0.109375 to 0.109375
- down_bias: bfloat16 [3, 768], P(None, 'tensor'), may hold values from -3 to 3
- norm_gain: bfloat16 [3, 2, 768], P(None, None, 'tensor'), may hold values from 0.099609375 to 1.8984375
- norm_bias: bfloat16 [3, 2, 768], P(None, None, 'tensor'), may hold values from -3 to 3
- image_upstream: bfloat16 [16, 197, 768], P('dp', None, 'tensor'), may hold values from -6 to 6
- text_upstream: bfloat16 [8, 512, 768], P('dp', None, 'tensor'), may hold values from -6 to 6
- pair_upstream: bfloat16 [8, 711, 768], P('dp', None, 'tensor'), may hold values from -6 to 6
Outputs:
- image_out: bfloat16 [16, 197, 768], P('dp', None, 'tensor')
- text_out: bfloat16 [8, 512, 768], P('dp', None, 'tensor')
- pair_out: bfloat16 [8, 711, 768], P('dp', None, 'tensor')
- image_input_grad: bfloat16 [16, 197, 768], P('dp', None, 'tensor')
- text_input_grad: bfloat16 [8, 512, 768], P('dp', None, 'tensor')
- pair_input_grad: bfloat16 [8, 711, 768], P('dp', None, 'tensor')
- qkv_grad: float32 [3, 768, 3, 768], P(None, 'dp', None, 'tensor')
- qv_bias_grad: float32 [3, 2, 768], P(None, None, 'tensor')
- out_weight_grad: float32 [3, 768, 768], P(None, 'tensor', 'dp')
- out_bias_grad: float32 [3, 768], P(None, 'tensor')
- up_weight_grad: float32 [3, 768, 3072], P(None, 'dp', 'tensor')
- up_bias_grad: float32 [3, 3072], P(None, 'tensor')
- down_weight_grad: float32 [3, 3072, 768], P(None, 'tensor', 'dp')
- down_bias_grad: float32 [3, 768], P(None, 'tensor')
- norm_gain_grad: float32 [3, 2, 768], P(None, None, 'tensor')
- norm_bias_grad: float32 [3, 2, 768], P(None, None, 'tensor')
Inputs may be any that keep to these rules, and one draw needn't show every extreme that they name: Each text example's first text_lengths rows of 512 are valid; some example of every draw has all 512. Each pair's text rows after its 197 image rows: the first pair_lengths are valid, the rest and the two pad rows are not; some pair of every draw has all 512.
All inputs are finite; a program needn't handle non-finite values.
Results may differ from a plain program's by a relative error of at most 0.017.
Values may be sent and summed in bfloat16 or wider, within the bound.
A program may use at most 192 MiB of HBM per device.

v0:
```python
import math
import jax
import jax.numpy as jnp
from jax import lax
from jax.sharding import PartitionSpec as P

HEAD_DIM = 64
PATCHES = 196
EPSILON = 1e-06


def rounded(value):
    return lax.optimization_barrier(value.astype(jnp.bfloat16)).astype(jnp.float32)


def moments(total_count, square, feature_width):
    mean_val = total_count / feature_width
    return (mean_val, lax.rsqrt(square / feature_width - mean_val * mean_val + EPSILON))


def local_moments(value, feature_width):
    return moments(
        jnp.sum(value, axis=-1, keepdims=True),
        jnp.sum(value * value, axis=-1, keepdims=True),
        feature_width,
    )


def gather_grads(value):
    return lax.all_gather(value, "tensor", axis=2, tiled=True)


def summed_grads(value):
    return lax.psum_scatter(
        rounded(value).astype(jnp.bfloat16), "tensor", scatter_dimension=2, tiled=True
    ).astype(jnp.float32)


def norm_reverse_pass(centered_grad, standardized, inverse_deviation, feature_width):
    total_count, cross_term = lax.psum(
        (
            jnp.sum(centered_grad, axis=-1, keepdims=True),
            jnp.sum(centered_grad * standardized, axis=-1, keepdims=True),
        ),
        "tensor",
    )
    return inverse_deviation * (
        centered_grad - total_count / feature_width - standardized * cross_term / feature_width
    )


def gelu_exact(value):
    return jax.nn.gelu(value, approximate=False)


def masked_scores(queries, key_heads, key_mask, scale):
    scores = (
        jnp.einsum("elhd,emhd->ehlm", queries, key_heads, preferred_element_type=jnp.float32)
        * scale
    )
    return jnp.where(key_mask[:, None, None, :], scores, -1000000000.0)


def forward_tower(row_block, key_mask, weights, tensor_index):
    qkv_w, qv_b, out_w, out_b, up_w, up_b, down_w, down_b, gain, shift = weights
    feature_width = qkv_w.shape[0]
    share = out_w.shape[0]
    examples = row_block.shape[0]
    length = row_block.shape[1]
    head_count = share // HEAD_DIM
    scale = 1.0 / math.sqrt(HEAD_DIM)
    rows_float = row_block.astype(jnp.float32)
    whole_rows, whole_bias, whole_gain, whole_shift = (
        lax.all_gather(row_block, "tensor", axis=2, tiled=True),
        lax.all_gather(out_b, "tensor", axis=0, tiled=True),
        lax.all_gather(gain, "tensor", axis=1, tiled=True),
        lax.all_gather(shift, "tensor", axis=1, tiled=True),
    )
    whole_f = whole_rows.astype(jnp.float32)
    input_mean, input_inverse_deviation = local_moments(whole_f, feature_width)
    normed = (
        (whole_f - input_mean) * input_inverse_deviation * whole_gain[0].astype(jnp.float32)
        + whole_shift[0].astype(jnp.float32)
    ).astype(jnp.bfloat16)
    projected = jnp.einsum("eld,dcf->elcf", normed, qkv_w, preferred_element_type=jnp.float32)
    queries = (
        (projected[:, :, 0] + qv_b[0].astype(jnp.float32))
        .astype(jnp.bfloat16)
        .reshape(examples, length, head_count, HEAD_DIM)
    )
    key_heads = (
        projected[:, :, 1].astype(jnp.bfloat16).reshape(examples, length, head_count, HEAD_DIM)
    )
    value_heads = (
        (projected[:, :, 2] + qv_b[1].astype(jnp.float32))
        .astype(jnp.bfloat16)
        .reshape(examples, length, head_count, HEAD_DIM)
    )
    scores = masked_scores(queries, key_heads, key_mask, scale)
    top_score = jnp.max(scores, axis=-1, keepdims=True)
    log_total = top_score + jnp.log(jnp.sum(jnp.exp(scores - top_score), axis=-1, keepdims=True))
    probs_low = jnp.exp(scores - log_total).astype(jnp.bfloat16)
    mixed = (
        jnp.einsum("ehlm,emhd->elhd", probs_low, value_heads, preferred_element_type=jnp.float32)
        .astype(jnp.bfloat16)
        .reshape(examples, length, share)
    )
    partial_value = jnp.einsum("elf,fd->eld", mixed, out_w, preferred_element_type=jnp.float32)
    attn_full = lax.psum(rounded(partial_value).astype(jnp.bfloat16), "tensor").astype(
        jnp.float32
    ) + whole_bias.astype(jnp.float32)
    resid_full = whole_f + attn_full
    middle_mean, middle_inverse_deviation = local_moments(resid_full, feature_width)
    normed_two = (
        (resid_full - middle_mean) * middle_inverse_deviation * whole_gain[1].astype(jnp.float32)
        + whole_shift[1].astype(jnp.float32)
    ).astype(jnp.bfloat16)
    attention = lax.dynamic_slice_in_dim(attn_full, tensor_index * share, share, 2)
    residual_stream = rows_float + attention
    hidden = jnp.einsum(
        "eld,df->elf", normed_two, up_w, preferred_element_type=jnp.float32
    ) + up_b.astype(jnp.float32)
    activated = gelu_exact(hidden).astype(jnp.bfloat16)
    down_part = jnp.einsum("elf,fd->eld", activated, down_w, preferred_element_type=jnp.float32)
    feedforward = lax.psum_scatter(
        rounded(down_part).astype(jnp.bfloat16), "tensor", scatter_dimension=2, tiled=True
    ).astype(jnp.float32) + down_b.astype(jnp.float32)
    output = residual_stream + feedforward
    kept = (
        normed,
        queries,
        key_heads,
        value_heads,
        log_total,
        mixed,
        normed_two,
        hidden,
        activated,
        input_mean,
        input_inverse_deviation,
        middle_mean,
        middle_inverse_deviation,
        residual_stream,
        rows_float,
    )
    return (output, kept)


def backward_tower(upstream, weights, kept, key_mask):
    qkv_w, qv_b, out_w, out_b, up_w, up_b, down_w, down_b, gain, shift = weights
    (
        normed,
        queries,
        key_heads,
        value_heads,
        log_total,
        mixed,
        normed_two,
        hidden,
        activated,
        input_mean,
        input_inverse_deviation,
        middle_mean,
        middle_inverse_deviation,
        residual_stream,
        rows_float,
    ) = kept
    feature_width = qkv_w.shape[0]
    share = out_w.shape[0]
    examples = queries.shape[0]
    length = queries.shape[1]
    head_count = share // HEAD_DIM
    scale = 1.0 / math.sqrt(HEAD_DIM)
    gain_float = gain.astype(jnp.float32)
    output_gradient = upstream.astype(jnp.float32)
    grad_ffn = output_gradient.astype(jnp.bfloat16)
    down_bias_grad = jnp.sum(grad_ffn, axis=(0, 1), dtype=jnp.float32)
    ffn_full = gather_grads(grad_ffn)
    down_grad = jnp.einsum("elf,eld->fd", activated, ffn_full, preferred_element_type=jnp.float32)
    grad_act = jnp.einsum("eld,fd->elf", ffn_full, down_w, preferred_element_type=jnp.float32)
    grad_hidden = jax.vjp(gelu_exact, hidden)[1](grad_act)[0].astype(jnp.bfloat16)
    up_bias_grad = jnp.sum(grad_hidden, axis=(0, 1), dtype=jnp.float32)
    up_grad = jnp.einsum("eld,elf->df", normed_two, grad_hidden, preferred_element_type=jnp.float32)
    second_normed_gradient = summed_grads(
        jnp.einsum("elf,df->eld", grad_hidden, up_w, preferred_element_type=jnp.float32)
    )
    standardized_middle = (residual_stream - middle_mean) * middle_inverse_deviation
    middle_gain_grad = jnp.sum(second_normed_gradient * standardized_middle, axis=(0, 1))
    shift_mid_grad = jnp.sum(second_normed_gradient, axis=(0, 1))
    residual_gradient = output_gradient + norm_reverse_pass(
        second_normed_gradient * gain_float[1],
        standardized_middle,
        middle_inverse_deviation,
        feature_width,
    )
    grad_attn = residual_gradient.astype(jnp.bfloat16)
    out_bias_grad = jnp.sum(grad_attn, axis=(0, 1), dtype=jnp.float32)
    attn_full = gather_grads(grad_attn)
    out_grad = jnp.einsum("elf,eld->fd", mixed, attn_full, preferred_element_type=jnp.float32)
    grad_mixed = (
        jnp.einsum("eld,fd->elf", attn_full, out_w, preferred_element_type=jnp.float32)
        .astype(jnp.bfloat16)
        .reshape(examples, length, head_count, HEAD_DIM)
    )
    scores = masked_scores(queries, key_heads, key_mask, scale)
    probs_f = jnp.exp(scores - log_total)
    probs_low = probs_f.astype(jnp.bfloat16)
    grad_values = jnp.einsum(
        "ehlm,elhd->emhd", probs_low, grad_mixed, preferred_element_type=jnp.float32
    ).astype(jnp.bfloat16)
    grad_probs = jnp.einsum(
        "elhd,emhd->ehlm", grad_mixed, value_heads, preferred_element_type=jnp.float32
    )
    grad_scores = (
        probs_f * (grad_probs - jnp.sum(probs_f * grad_probs, axis=-1, keepdims=True))
    ).astype(jnp.bfloat16)
    grad_queries = (
        jnp.einsum("ehlm,emhd->elhd", grad_scores, key_heads, preferred_element_type=jnp.float32)
        * scale
    ).astype(jnp.bfloat16)
    grad_keys = (
        jnp.einsum("ehlm,elhd->emhd", grad_scores, queries, preferred_element_type=jnp.float32)
        * scale
    ).astype(jnp.bfloat16)
    grad_qkv = jnp.stack([grad_queries, grad_keys, grad_values], 2).reshape(
        examples, length, 3, share
    )
    qv_bias_grad = jnp.stack(
        [
            jnp.sum(grad_qkv[:, :, 0], axis=(0, 1), dtype=jnp.float32),
            jnp.sum(grad_qkv[:, :, 2], axis=(0, 1), dtype=jnp.float32),
        ],
        0,
    )
    qkv_grad = jnp.einsum("eld,elcf->dcf", normed, grad_qkv, preferred_element_type=jnp.float32)
    normed_gradient = summed_grads(
        jnp.einsum("elcf,dcf->eld", grad_qkv, qkv_w, preferred_element_type=jnp.float32)
    )
    standardized_input = (rows_float - input_mean) * input_inverse_deviation
    input_gain_grad = jnp.sum(normed_gradient * standardized_input, axis=(0, 1))
    shift_in_grad = jnp.sum(normed_gradient, axis=(0, 1))
    grad_input = (
        residual_gradient
        + norm_reverse_pass(
            normed_gradient * gain_float[0],
            standardized_input,
            input_inverse_deviation,
            feature_width,
        )
    ).astype(jnp.bfloat16)
    small_grads = jnp.concatenate(
        [
            qv_bias_grad,
            out_bias_grad[None],
            up_bias_grad.reshape(-1, share),
            down_bias_grad[None],
            jnp.stack([input_gain_grad, middle_gain_grad], 0),
            jnp.stack([shift_in_grad, shift_mid_grad], 0),
        ],
        0,
    )
    return (grad_input, (qkv_grad, out_grad, up_grad, down_grad, small_grads))


def per_device(
    image_rows,
    text_rows,
    pair_rows,
    text_lengths,
    pair_lengths,
    qkv_weight,
    qv_bias,
    out_weight,
    out_bias,
    up_weight,
    up_bias,
    down_weight,
    down_bias,
    norm_gain,
    norm_bias,
    image_upstream,
    text_upstream,
    pair_upstream,
):
    tensor_index = lax.axis_index("tensor")
    image_mask = jnp.ones((image_rows.shape[0], image_rows.shape[1]), dtype=bool)
    text_mask = jnp.arange(text_rows.shape[1], dtype=jnp.int32)[None, :] < text_lengths[:, None]
    pair_mask = jnp.arange(pair_rows.shape[1], dtype=jnp.int32)[None, :] < pair_lengths[:, None] + (
        PATCHES + 1
    )
    towers_in = (
        (image_rows, image_mask, image_upstream),
        (text_rows, text_mask, text_upstream),
        (pair_rows, pair_mask, pair_upstream),
    )
    params = (
        qkv_weight,
        qv_bias,
        out_weight,
        out_bias,
        up_weight,
        up_bias,
        down_weight,
        down_bias,
        norm_gain,
        norm_bias,
    )
    outputs = []
    input_grads = []
    grad_lists = ([], [], [], [], [])
    for tower_id in range(3):
        row_block, key_mask, upstream = towers_in[tower_id]
        weights = tuple((entry[tower_id] for entry in params))
        output, kept = forward_tower(row_block, key_mask, weights, tensor_index)
        outputs.append(output.astype(jnp.bfloat16))
        grad_input, grads = backward_tower(upstream, weights, kept, key_mask)
        input_grads.append(grad_input)
        for slot_id in range(5):
            grad_lists[slot_id].append(grads[slot_id])
    stacked = tuple((jnp.stack(group_list, 0) for group_list in grad_lists))
    qkv_grad, out_weight_grad, up_weight_grad, down_weight_grad = (
        lax.psum_scatter(stacked[0], "dp", scatter_dimension=1, tiled=True),
        lax.psum_scatter(stacked[1], "dp", scatter_dimension=2, tiled=True),
        lax.psum_scatter(stacked[2], "dp", scatter_dimension=1, tiled=True),
        lax.psum_scatter(stacked[3], "dp", scatter_dimension=2, tiled=True),
    )
    small_grads = lax.psum(stacked[4], "dp")
    share = out_weight.shape[1]
    hidden_share = up_weight.shape[2]
    ratio = hidden_share // share
    qv_bias_grad = small_grads[:, 0:2]
    out_bias_grad = small_grads[:, 2]
    up_bias_grad = small_grads[:, 3 : 3 + ratio].reshape(3, hidden_share)
    down_bias_grad = small_grads[:, 3 + ratio]
    norm_gain_grad = small_grads[:, 4 + ratio : 6 + ratio]
    norm_bias_grad = small_grads[:, 6 + ratio : 8 + ratio]
    return (
        outputs[0],
        outputs[1],
        outputs[2],
        input_grads[0],
        input_grads[1],
        input_grads[2],
        qkv_grad,
        qv_bias_grad,
        out_weight_grad,
        out_bias_grad,
        up_weight_grad,
        up_bias_grad,
        down_weight_grad,
        down_bias_grad,
        norm_gain_grad,
        norm_bias_grad,
    )


def solution(mesh):
    return jax.shard_map(
        per_device,
        mesh=mesh,
        in_specs=(
            P("dp", None, "tensor"),
            P("dp", None, "tensor"),
            P("dp", None, "tensor"),
            P("dp"),
            P("dp"),
            P(None, None, None, "tensor"),
            P(None, None, "tensor"),
            P(None, "tensor", None),
            P(None, "tensor"),
            P(None, None, "tensor"),
            P(None, "tensor"),
            P(None, "tensor", None),
            P(None, "tensor"),
            P(None, None, "tensor"),
            P(None, None, "tensor"),
            P("dp", None, "tensor"),
            P("dp", None, "tensor"),
            P("dp", None, "tensor"),
        ),
        out_specs=(
            P("dp", None, "tensor"),
            P("dp", None, "tensor"),
            P("dp", None, "tensor"),
            P("dp", None, "tensor"),
            P("dp", None, "tensor"),
            P("dp", None, "tensor"),
            P(None, "dp", None, "tensor"),
            P(None, None, "tensor"),
            P(None, "tensor", "dp"),
            P(None, "tensor"),
            P(None, "dp", "tensor"),
            P(None, "tensor"),
            P(None, "tensor", "dp"),
            P(None, "tensor"),
            P(None, None, "tensor"),
            P(None, None, "tensor"),
        ),
        check_vma=False,
    )
```

profile of v0, /device:TPU:0, one launch (start us, length us, event | category | flops | bytes accessed | tf_op | source)
XLA Modules:
  0.0 1013.4 jit_solution(11684703509112066378)
XLA Ops:
  8.7 7.9 all-gather.1
  16.7 5.3 fusion.178
  23.4 6.6 all-gather
  30.0 5.3 fusion.179
  35.5 8.7 all_gather.54
  56.0 12.3 %all_gather.58 = bf16[1,512,768]{1,2,0:T(8,128)(2,1)S(1)} all-gather(bf16[1,512,192]{1,2,0:T(8,128)(2,1)S(1)} %copy-done.81), channel_id=1, replica_groups=mesh['dp'=8,'tensor'=4] {'tensor'}, dimensions={2}, use_global_device_ids=true | all-gather | bytes 983040 | tf_op jit(solution)/shard_map/all_gather | solution.py:74
  68.7 6.6 all-gather.4
  75.3 5.3 fusion.174
  80.8 8.5 all-gather.3
  89.3 5.3 fusion.175
  100.1 8.3 all-reduce.8
  122.7 6.1 all-gather.7
  128.8 4.7 fusion.170
  133.7 6.6 all-gather.6
  140.3 4.7 fusion.171
  145.3 9.7 all_gather.66
  160.3 3.6 multiply_convert_fusion.5
  163.9 2.9 convert_reduce_fusion.5
  170.4 3.0 copy.174
  192.1 10.5 %all_gather.68 = bf16[1,512,768]{1,2,0:T(8,128)(2,1)} all-gather(bf16[1,512,192]{1,2,0:T(8,128)(2,1)S(1)} %copy-done.82), channel_id=1, replica_groups=mesh['dp'=8,'tensor'=4] {'tensor'}, dimensions={2}, use_global_device_ids=true | all-gather | bytes 983040 | tf_op jit(solution)/shard_map/all_gather | solution.py:30
  202.6 51.6 %all-reduce.19.cloned.1.call-done = (bf16[1,512,768]{2,1,0:T(8,128)(2,1)}, bf16[1,711,768]{2,1,0:T(8,128)(2,1)}, bf16[2,197,768]{1,0,2:T(2,128)(2,1)}) async-done(((bf16[1,512,768]{2,1,0:T(8,128)(2,1)}, bf16[1,711,768]{2,1,0:T(8,128)(2,1)}, bf16[2,197,768]{1,0,2:T(2,128)(2,1)}), (bf16[1,512,768]{2,1,0:T(8,128)(2,1)}, bf16[1,711,768]{2,1,0:T(8,128)(2,1)}, ...) | async-done | bytes 2483728 | tf_op jit(solution)/shard_map/psum | solution.py:109
  254.2 3.0 fusion.133
  257.3 6.4 multiply_convert_fusion.3
  263.7 3.1 convert_reduce_fusion.4
  267.6 3.0 fusion.34
  270.6 4.7 copy.225
  277.9 3.2 fusion.33
  281.1 4.8 copy.221
  290.5 9.1 multiply_convert_fusion.2
  299.6 5.4 convert_reduce_fusion.2
  306.0 3.3 fusion.28
  309.3 6.7 copy.229
  316.0 2.9 copy.269
  332.4 4.5 slice_reduce_fusion.4
  336.9 4.5 slice_reduce_fusion.2
  341.4 4.5 slice_reduce_fusion
  346.6 2.9 convolution_convert_fusion.7
  349.5 3.0 copy.161
  356.0 3.6 fusion.27
  359.6 6.7 copy.223
  366.3 2.9 copy.270
  389.0 11.6 %all-reduce.7 = (f32[2,197]{1,0:T(2,128)}, f32[2,197,1]{1,0,2:T(2,128)}, f32[512]{0:T(512)}, f32[1,512,1]{1,2,0:T(1,128)}, f32[711]{0:T(1024)}, /*index=5*/f32[1,711,1]{1,2,0:T(1,128)}) all-reduce(f32[2,197]{1,0:T(2,128)} %get-tuple-element.87, f32[2,197,1]{1,0,2:T(2,128)} %bitcast.503, ...), channel_id=1, replica_groups=mesh['dp'=8,'tensor'=4] {'tensor'}, use_global_device_ids=true, to_apply=%region_28.29 | all-reduce | flops 3234 | bytes 25872 | tf_op jit(solution)/shard_map/psum | solution.py:40
  401.2 3.0 convert_reduce_fusion.19
  406.0 9.1 all_gather.67
  424.3 3.0 copy.184
  427.3 3.6 convert_reduce_fusion.17
  437.5 4.1 convert_reduce_fusion.11
  443.5 9.0 all_gather.69
  464.2 2.9 copy.227
  473.2 5.3 multiply_reduce_fusion
  485.8 2.8 copy.231
  493.5 3.0 copy.235
  496.5 2.8 reshape.1243
  504.3 3.3 pad_maximum_fusion.1
  507.6 11.0 %copy.237 = f32[3,768,768]{1,0,2:T(4,128)} copy(f32[3,768,768]{2,1,0:T(8,128)} %pad_maximum_fusion.1) | data formatting | bytes 14155776
  518.5 8.2 copy.255
  535.6 9.8 copy.233
  545.4 11.3 %reshape.1241 = f32[768,1728]{1,0:T(8,128)} reshape(f32[768,3,3,192]{3,2,1,0:T(4,128)} %bitcast.422) | data formatting | bytes 10616832
  563.0 3.4 pad_maximum_fusion
  577.5 10.9 %all-reduce.6 = (f32[2,197]{1,0:T(2,128)S(1)}, f32[2,197,1]{1,0,2:T(2,128)S(1)}, f32[512]{0:T(512)S(1)}, f32[1,512,1]{1,2,0:T(1,128)S(1)}, f32[711]{0:T(1024)S(1)}, /*index=5*/f32[1,711,1]{1,2,0:T(1,128)S(1)}) all-reduce(f32[2,197]{1,0:T(2,128)S(1)} %get-tuple-element.105, ...), channel_id=1, replica_groups=mesh['dp'=8,'tensor'=4] {'tensor'}, use_global_device_ids=true, to_apply=%region_34.35 | all-reduce | flops 3234 | bytes 25872 | tf_op jit(solution)/shard_map/psum | solution.py:40
  597.3 38.3 %psum.127 = f32[3,12,192]{2,1,0:T(8,128)S(1)} all-reduce(f32[3,12,192]{2,1,0:T(8,128)S(1)} %pad_maximum_fusion.9), channel_id=1, replica_groups=mesh['dp'=8,'tensor'=4] {'dp'}, use_global_device_ids=true, to_apply=%region_85.86 | all-reduce | flops 6912 | bytes 55296 | tf_op jit(solution)/shard_map/psum | solution.py:327
  639.6 124.9 %reduce-scatter.47.cloned.1.call-done = f32[96,2304]{1,0:T(8,128)} async-done(((f32[768,2304]{1,0:T(8,128)}), f32[96,2304]{1,0:T(8,128)}) %reduce-scatter.47.cloned.1.call-update) | async-done | bytes 884752
  767.2 106.9 %reduce-scatter.43.cloned.1.call-done = f32[96,1728]{1,0:T(8,128)} async-done(((f32[768,1728]{1,0:T(8,128)}), f32[96,1728]{1,0:T(8,128)}) %reduce-scatter.43.cloned.1.call-update) | async-done | bytes 663568
  876.9 129.8 %reduce-scatter.29.cloned.1.call-done = f32[3,96,768]{2,1,0:T(8,128)} async-done(((f32[3,768,768]{2,1,0:T(8,128)}), f32[3,96,768]{2,1,0:T(8,128)}) %reduce-scatter.29.cloned.1.call-update) | async-done | bytes 884752 | tf_op jit(solution)/shard_map/reduce_scatter | solution.py:324
  (684 shorter events, 204.2 us)
Async XLA Ops:
  7.2 28.1 %copy-start.77 = (bf16[2,197,192]{1,2,0:T(8,128)(2,1)S(1)}, bf16[2,197,192]{1,2,0:T(8,128)(2,1)}, u32[]{:S(2)}) copy-start(bf16[2,197,192]{1,2,0:T(8,128)(2,1)} %param.18) | copy-start | bytes 453892
  7.2 147.8 %all-reduce.15.cloned.1.call-start = ((), (), s32[]{:S(2)}) async-start(), calls=%async_computation.10 | async-start | bytes 1228800 | tf_op jit(solution)/shard_map/psum | solution.py:109
  22.0 23.2 %copy-start.166 = (f32[768]{0:T(1024)}, f32[768]{0:T(1024)S(1)}, u32[]{:S(2)}) copy-start(f32[768]{0:T(1024)S(1)} %get-tuple-element.116) | copy-start | bytes 9220
  23.4 12.1 %copy-start.66 = (bf16[1,2,192]{1,0,2:T(2,128)(2,1)}, bf16[1,2,192]{1,0,2:T(2,128)(2,1)S(1)}, u32[]{:S(2)}) copy-start(bf16[1,2,192]{1,0,2:T(2,128)(2,1)S(1)} %copy.249) | copy-start | bytes 2308
  35.3 9.8 copy-start.168
  52.7 120.8 %all-gather.13.cloned.1.call-start = ((), (), s32[]{:S(2)}) async-start(), calls=%async_computation.11 | async-start | bytes 1474560 | tf_op jit(solution)/shard_map/all_gather | solution.py:74
  53.4 200.8 %all-reduce.19.cloned.1.call-start = ((), (), s32[]{:S(2)}) async-start(), calls=%async_computation.25 | async-start | bytes 5332992 | tf_op jit(solution)/shard_map/psum | solution.py:109
  68.6 26.4 %copy-start.11 = (bf16[1,512,768]{2,1,0:T(8,128)(2,1)}, bf16[1,512,768]{2,1,0:T(8,128)(2,1)S(1)}, u32[]{:S(2)}) copy-start(bf16[1,512,768]{2,1,0:T(8,128)(2,1)S(1)} %copy.164) | copy-start | bytes 2359300
  80.6 15.3 %copy-start.174 = (f32[768]{0:T(1024)}, f32[768]{0:T(1024)S(1)}, u32[]{:S(2)}) copy-start(f32[768]{0:T(1024)S(1)} %get-tuple-element.112) | copy-start | bytes 9220
  80.8 15.1 %copy-start.68 = (bf16[1,2,192]{1,0,2:T(2,128)(2,1)}, bf16[1,2,192]{1,0,2:T(2,128)(2,1)S(1)}, u32[]{:S(2)}) copy-start(bf16[1,2,192]{1,0,2:T(2,128)(2,1)S(1)} %copy.251) | copy-start | bytes 2308
  97.4 14.2 %copy-start.25 = (f32[1,512,1,192]{1,3,2,0:T(8,128)}, f32[1,512,1,192]{1,3,2,0:T(8,128)S(1)}, u32[]{:S(2)}) copy-start(f32[1,512,1,192]{1,3,2,0:T(8,128)S(1)} %get-tuple-element.191) | copy-start | bytes 1179652
  118.2 15.4 %copy-start.199 = (bf16[1,2,192]{2,1,0:T(2,128)(2,1)S(1)}, bf16[1,2,192]{2,1,0:T(2,128)(2,1)}, u32[]{:S(2)}) copy-start(bf16[1,2,192]{2,1,0:T(2,128)(2,1)} %get-tuple-element.209) | copy-start | bytes 2308
  121.1 24.0 %copy-start.203 = (f32[192]{0:T(256)S(1)}, f32[192]{0:T(256)}, u32[]{:S(2)}) copy-start(f32[192]{0:T(256)} %get-tuple-element.144) | copy-start | bytes 2308
  121.1 24.1 %copy-start.202 = (f32[192]{0:T(256)S(1)}, f32[192]{0:T(256)}, u32[]{:S(2)}) copy-start(f32[192]{0:T(256)} %get-tuple-element.139) | copy-start | bytes 2308
  121.1 24.1 %copy-start.83 = (bf16[2,197,192]{1,2,0:T(8,128)(2,1)S(1)}, bf16[2,197,192]{1,2,0:T(8,128)(2,1)}, u32[]{:S(2)}) copy-start(bf16[2,197,192]{1,2,0:T(8,128)(2,1)} %param.33) | copy-start | bytes 453892
  121.8 61.7 %copy-start.110 = (pred[711]{0:T(1024)(128)(4,1)}, pred[711]{0:T(1024)(128)(4,1)S(1)}, u32[]{:S(2)}) copy-start(pred[711]{0:T(1024)(128)(4,1)S(1)} %iota_compare_fusion) | copy-start | bytes 2137
  128.8 26.2 %copy-start.140 = (f32[768]{0:T(1024)S(1)}, f32[768]{0:T(1024)}, u32[]{:S(2)}) copy-start(f32[768]{0:T(1024)} %convert_element_type.887) | copy-start | bytes 9220
  133.5 44.0 %copy-start.182 = (f32[768]{0:T(1024)}, f32[768]{0:T(1024)S(1)}, u32[]{:S(2)}) copy-start(f32[768]{0:T(1024)S(1)} %get-tuple-element.108) | copy-start | bytes 9220
  133.5 156.9 %copy-start.178 = (f32[768]{0:T(1024)}, f32[768]{0:T(1024)S(1)}, u32[]{:S(2)}) copy-start(f32[768]{0:T(1024)S(1)} %get-tuple-element.109) | copy-start | bytes 9220
  133.7 24.0 %copy-start.70 = (bf16[1,2,192]{1,0,2:T(2,128)(2,1)}, bf16[1,2,192]{1,0,2:T(2,128)(2,1)S(1)}, u32[]{:S(2)}) copy-start(bf16[1,2,192]{1,0,2:T(2,128)(2,1)S(1)} %copy.253) | copy-start | bytes 2308
  145.0 32.5 %copy-start.184 = (f32[768]{0:T(1024)}, f32[768]{0:T(1024)S(1)}, u32[]{:S(2)}) copy-start(f32[768]{0:T(1024)S(1)} %get-tuple-element.106) | copy-start | bytes 9220
  145.1 145.4 %copy-start.180 = (f32[768]{0:T(1024)}, f32[768]{0:T(1024)S(1)}, u32[]{:S(2)}) copy-start(f32[768]{0:T(1024)S(1)} %get-tuple-element.107) | copy-start | bytes 9220
  145.2 35.2 %copy-start.134 = (f32[3,64]{1,0:T(4,128)}, f32[3,64]{1,0:T(4,128)S(1)}, u32[]{:S(2)}) copy-start(f32[3,64]{1,0:T(4,128)S(1)} %reshape.1120) | copy-start | bytes 2308
  145.2 41.0 %copy-start.136 = (f32[3,64]{1,0:T(4,128)}, f32[3,64]{1,0:T(4,128)S(1)}, u32[]{:S(2)}) copy-start(f32[3,64]{1,0:T(4,128)S(1)} %reshape.1119) | copy-start | bytes 2308
  145.3 12.5 %copy-start.162 = (f32[768]{0:T(1024)S(1)}, f32[768]{0:T(1024)}, u32[]{:S(2)}) copy-start(f32[768]{0:T(1024)} %get-tuple-element.117) | copy-start | bytes 9220
  145.3 12.5 %copy-start.164 = (f32[768]{0:T(1024)S(1)}, f32[768]{0:T(1024)}, u32[]{:S(2)}) copy-start(f32[768]{0:T(1024)} %get-tuple-element.115) | copy-start | bytes 9220
  145.3 12.5 %copy-start.209 = (f32[768]{0:T(1024)S(1)}, f32[768]{0:T(1024)}, u32[]{:S(2)}) copy-start(f32[768]{0:T(1024)} %get-tuple-element.137) | copy-start | bytes 9220
  191.2 108.4 %all-gather.15.cloned.1.call-start = ((), (), s32[]{:S(2)}) async-start(), calls=%async_computation.12 | async-start | bytes 1474560 | tf_op jit(solution)/shard_map/all_gather | solution.py:30
  191.8 179.9 %reduce-scatter.35.cloned.1.call-start = ((), (), s32[]{:S(2)}) async-start(), calls=%async_computation.17 | async-start | bytes 983040
  192.1 65.1 %copy-start.142 = (f32[768]{0:T(1024)}, f32[768]{0:T(1024)S(1)}, u32[]{:S(2)}) copy-start(f32[768]{0:T(1024)S(1)} %convert_element_type.888) | copy-start | bytes 9220
  277.9 97.5 %reduce-scatter.31.cloned.1.call-start = ((), (), s32[]{:S(2)}) async-start(), calls=%async_computation.15 | async-start | bytes 983040
  277.9 12.6 %copy-start.144 = (f32[768]{0:T(1024)}, f32[768]{0:T(1024)S(1)}, u32[]{:S(2)}) copy-start(f32[768]{0:T(1024)S(1)} %convert_element_type.889) | copy-start | bytes 9220
  290.4 9.2 copy-start.98
  290.4 9.2 copy-start.101
  290.4 91.2 %reduce-scatter.39.cloned.1.call-start = ((), (), s32[]{:S(2)}) async-start(), calls=%async_computation.19 | async-start | bytes 1474560
  318.9 114.5 %reduce-scatter.33.cloned.1.call-start = ((), (), s32[]{:S(2)}) async-start(), calls=%async_computation.16 | async-start | bytes 1474560
  322.7 23.3 %copy-start.161 = (bf16[3,192]{1,0:T(4,128)(2,1)S(1)}, bf16[3,192]{1,0:T(4,128)(2,1)}, u32[]{:S(2)}) copy-start(bf16[3,192]{1,0:T(4,128)(2,1)} %param.30) | copy-start | bytes 3460
  324.6 112.9 %copy-start.9 = (bf16[1,711,192]{2,1,0:T(8,128)(2,1)}, bf16[1,711,192]{2,1,0:T(8,128)(2,1)S(1)}, u32[]{:S(2)}) copy-start(bf16[1,711,192]{2,1,0:T(8,128)(2,1)S(1)} %copy.168) | copy-start | bytes 819076
  336.9 32.3 %copy-start.138 = (f32[192]{0:T(256)}, f32[192]{0:T(256)S(1)}, u32[]{:S(2)}) copy-start(f32[192]{0:T(256)S(1)} %get-tuple-element.135) | copy-start | bytes 2308
  369.2 100.9 %all-gather.17.cloned.1.call-start = ((), (), s32[]{:S(2)}) async-start(), calls=%async_computation.13 | async-start | bytes 1474560 | tf_op jit(solution)/shard_map/all_gather | solution.py:30
  369.3 9.8 copy-start.128
  369.3 9.8 copy-start.131
  371.7 7.5 copy-start.153
  401.2 15.3 %copy-start.121 = (f32[2,197]{1,0:T(2,128)}, f32[2,197]{1,0:T(2,128)S(1)}, u32[]{:S(2)}) copy-start(f32[2,197]{1,0:T(2,128)S(1)} %multiply_bitcast_fusion.1) | copy-start | bytes 4732
  406.0 10.6 %copy-start.2 = (f32[2,3,197,197]{2,3,1,0:T(8,128)S(1)}, f32[2,3,197,197]{2,3,1,0:T(8,128)}, u32[]{:S(2)}) copy-start(f32[2,3,197,197]{2,3,1,0:T(8,128)} %copy-done.1) | copy-start | bytes 2794252
  406.0 10.6 %copy-start.32 = (f32[2,197,1,192]{1,3,2,0:T(8,128)S(1)}, f32[2,197,1,192]{1,3,2,0:T(8,128)}, u32[]{:S(2)}) copy-start(f32[2,197,1,192]{1,3,2,0:T(8,128)} %copy-done.31) | copy-start | bytes 907780
  430.9 6.6 copy-start.186
  430.9 6.6 copy-start.200
  443.5 125.9 %all-reduce.17.cloned.1.call-start = ((), (), s32[]{:S(2)}) async-start(), calls=%async_computation.24 | async-start | bytes 3145728
  443.5 11.4 %copy-start.5 = (bf16[3,512,512]{1,2,0:T(8,128)(2,1)S(1)}, bf16[3,512,512]{1,2,0:T(8,128)(2,1)}, u32[]{:S(2)}) copy-start(bf16[3,512,512]{1,2,0:T(8,128)(2,1)} %fusion.14) | copy-start | bytes 4718596
  459.6 112.8 %reduce-scatter.37.cloned.1.call-start = ((), (), s32[]{:S(2)}) async-start(), calls=%async_computation.18 | async-start | bytes 983040
  469.9 104.9 %reduce-scatter.41.cloned.1.call-start = ((), (), s32[]{:S(2)}) async-start(), calls=%async_computation.20 | async-start | bytes 1474560
  473.2 9.7 copy-start.58
  489.9 147.6 %reduce-scatter.45.cloned.1.call-start = ((), (), s32[]{:S(2)}) async-start(), calls=%async_computation.22 | async-start | bytes 2211840
  499.4 265.1 %reduce-scatter.47.cloned.1.call-start = ((), (), s32[]{:S(2)}) async-start(), calls=%async_computation.23 | async-start | bytes 7962624
  526.8 347.3 %reduce-scatter.43.cloned.1.call-start = ((), (), s32[]{:S(2)}) async-start(), calls=%async_computation.21 | async-start | bytes 6193152
  556.8 449.9 %reduce-scatter.29.cloned.1.call-start = ((), (), s32[]{:S(2)}) async-start(), calls=%async_computation.14 | async-start | bytes 7962624 | tf_op jit(solution)/shard_map/reduce_scatter | solution.py:324
  574.0 14.4 %copy-start.35 = (bf16[2,197,192]{2,1,0:T(8,128)(2,1)S(1)}, bf16[2,197,192]{2,1,0:T(8,128)(2,1)}, u32[]{:S(2)}) copy-start(bf16[2,197,192]{2,1,0:T(8,128)(2,1)} %copy.175) | copy-start | bytes 453892
  574.0 14.4 %copy-start.47 = (bf16[2,197,192]{2,1,0:T(8,128)(2,1)S(1)}, bf16[2,197,192]{2,1,0:T(8,128)(2,1)}, u32[]{:S(2)}) copy-start(bf16[2,197,192]{2,1,0:T(8,128)(2,1)} %copy.173) | copy-start | bytes 453892
  574.0 14.4 %copy-start.122 = (f32[2,197]{1,0:T(2,128)S(1)}, f32[2,197]{1,0:T(2,128)}, u32[]{:S(2)}) copy-start(f32[2,197]{1,0:T(2,128)} %copy-done.121) | copy-start | bytes 4732
  574.0 14.4 %copy-start.139 = (f32[192]{0:T(256)S(1)}, f32[192]{0:T(256)}, u32[]{:S(2)}) copy-start(f32[192]{0:T(256)} %copy-done.138) | copy-start | bytes 2308
  574.1 14.4 %copy-start.159 = (f32[2,197]{1,0:T(2,128)S(1)}, f32[2,197]{1,0:T(2,128)}, u32[]{:S(2)}) copy-start(f32[2,197]{1,0:T(2,128)} %get-tuple-element.154) | copy-start | bytes 4732
  574.1 14.4 %copy-start.198 = (f32[1,192]{1,0:T(1,128)S(1)}, f32[1,192]{1,0:T(1,128)}, u32[]{:S(2)}) copy-start(f32[1,192]{1,0:T(1,128)} %get-tuple-element.216) | copy-start | bytes 2308
  576.9 17.7 %copy-start.46 = (f32[1,512,192]{2,1,0:T(8,128)S(1)}, f32[1,512,192]{2,1,0:T(8,128)}, u32[]{:S(2)}) copy-start(f32[1,512,192]{2,1,0:T(8,128)} %get-tuple-element.172) | copy-start | bytes 1179652
  (176 other events, 409.9 us)
Sparse Core Ops, SparseCore 0:
  52.8 36.7 all-reduce.14
  91.1 18.1 all-gather.12
  191.3 62.8 all-reduce.18
  255.6 17.4 all-gather.14
  278.0 23.3 reduce-scatter.34
  303.8 23.2 reduce-scatter.30
  329.6 25.6 reduce-scatter.38
  369.3 25.7 reduce-scatter.32
  443.6 17.4 all-gather.16
  464.5 42.8 all-reduce.16
  509.9 23.2 reduce-scatter.36
  535.6 25.6 reduce-scatter.40
  564.8 67.8 reduce-scatter.44
  636.2 128.2 reduce-scatter.46
  768.0 106.0 reduce-scatter.42
  878.2 128.5 reduce-scatter.28
where the time goes:
time: 1030 us; the launch traced here: 1010 us
  waiting for transfers between devices  415 us (40%)
  local copies, waits for them, and re-layouts  204 us (20%)
  blocking collectives  171 us (17%)
  matrix products  106 us (10%)
  other arithmetic  96.2 us (9%)
  between operations  19.5 us (2%)
    unnamed x26, waiting for transfers between devices  233 us
    unnamed x514, local copies, waits for them, and re-layouts  160 us
    reduce_scatter x1, waiting for transfers between devices, per_device(): lax.psum_scatter(stacked[2], 'dp', scatter_dimension=1, tiled=True)  130 us
    psum x2, waiting for transfers between devices, forward_tower(): lax.psum(rounded(partial_value).astype(jnp.bfloat16), 'tensor')  51.6 us
    all_gather x4, blocking collectives, gather_grads(): return lax.all_gather(value, 'tensor', axis=2, tiled=True)  38.4 us
    psum x1, blocking collectives, per_device(): small_grads = lax.psum(stacked[4], 'dp')  38.3 us
    psum x2, blocking collectives, norm_reverse_pass(): lax.psum((jnp.sum(centered_grad, axis=-1, keepdims=True), jnp.sum(centere...  22.5 us
    all_gather x3, blocking collectives, forward_tower(): lax.all_gather(gain, 'tensor', axis=1, tiled=True)  21.7 us
  transfers between devices with their start and end apart: 16, of which 4 were waited for; matrix products, arithmetic and copies ran while one was open for 34% of the time, Pallas kernels for 0%

commit v1 on v0

--- a/solution.py
+++ b/solution.py
@@ -70,10 +70,27 @@
     head_count = share // HEAD_DIM
     scale = 1.0 / math.sqrt(HEAD_DIM)
     rows_float = row_block.astype(jnp.float32)
+
+    def keep_up_boxes_for(array_here, pos_dim):
+        res, tmp, y_new = (
+            lax.axis_size("tensor"),
+            lax.axis_index("tensor"),
+            array_here.shape[pos_dim],
+        )
+        y2, found_now = (array_here, 1)
+        while found_now < res:
+            fields = []
+            for i0 in [*range(res)]:
+                fields.append((i0, (i0 - found_now) % res))
+            y2 = jnp.concatenate([y2, lax.ppermute(y2, "tensor", fields)], pos_dim)
+            found_now = 2 * found_now
+        vec_out = jnp.roll(y2, tmp * y_new, pos_dim)
+        return vec_out
+
     whole_rows, whole_bias, whole_gain, whole_shift = (
         lax.all_gather(row_block, "tensor", axis=2, tiled=True),
         lax.all_gather(out_b, "tensor", axis=0, tiled=True),
-        lax.all_gather(gain, "tensor", axis=1, tiled=True),
+        keep_up_boxes_for(gain, 1),
         lax.all_gather(shift, "tensor", axis=1, tiled=True),
     )
     whole_f = whole_rows.astype(jnp.float32)

time: 1030 us -> 980 us (0.951)
  blocking collectives: 171 us -> 152 us
  local copies, waits for them, and re-layouts: 204 us -> 189 us
  other arithmetic: 96.2 us -> 82.5 us
  waiting for transfers between devices: 415 us -> 404 us
    all_gather x3 -> x0, blocking collectives: 21.7 us -> none  [forward_tower(): lax.all_gather(gain, 'tensor', axis=1, tiled=True)]
    convert_element_type x3, other arithmetic: 15.3 us -> 1.84 us  [forward_tower(): whole_gain[0].astype(jnp.float32)]
    unnamed x26, waiting for transfers between devices: 233 us -> 220 us
    slice x3 -> x2, local copies, waits for them, and re-layouts: 13.6 us -> 1.18 us  [backward_tower(): gain_float[0]]
    unnamed x514 -> x488, local copies, waits for them, and re-layouts: 160 us -> 160 us
  transfers between devices with their start and end apart: 16 -> 22, of which waited for: 4 -> 6; matrix products, arithmetic and copies ran while one was open for 34% -> 34% of each run, Pallas kernels for 0% -> 0%
where the time goes in v1:
time: 980 us; the launch traced here: 969 us
  waiting for transfers between devices  404 us (41%)
  local copies, waits for them, and re-layouts  189 us (19%)
  blocking collectives  152 us (16%)
  matrix products  114 us (12%)
  other arithmetic  82.5 us (8%)
  between operations  19.6 us (2%)
    unnamed x26, waiting for transfers between devices  220 us
    unnamed x488, local copies, waits for them, and re-layouts  160 us
    reduce_scatter x1, waiting for transfers between devices, per_device(): lax.psum_scatter(stacked[2], 'dp', scatter_dimension=1, tiled=True)  130 us
    psum x2, waiting for transfers between devices, forward_tower(): lax.psum(rounded(partial_value).astype(jnp.bfloat16), 'tensor')  51 us
    all_gather x4, blocking collectives, gather_grads(): return lax.all_gather(value, 'tensor', axis=2, tiled=True)  41.5 us
    psum x1, blocking collectives, per_device(): small_grads = lax.psum(stacked[4], 'dp')  38.5 us
    psum x2, blocking collectives, norm_reverse_pass(): lax.psum((jnp.sum(centered_grad, axis=-1, keepdims=True), jnp.sum(centere...  23.1 us
    all_gather x2, blocking collectives, forward_tower(): lax.all_gather(row_block, 'tensor', axis=2, tiled=True)  21.3 us
  transfers between devices with their start and end apart: 22, of which 6 were waited for; matrix products, arithmetic and copies ran while one was open for 34% of the time, Pallas kernels for 0%

profile of v1, /device:TPU:0, one launch (start us, length us, event | category | flops | bytes accessed | tf_op | source)
XLA Modules:
  0.0 968.7 jit_solution(3763269037751807765)
XLA Ops:
  11.8 6.1 all-gather
  19.1 8.7 all_gather.45
  28.7 5.3 fusion.173
  50.3 12.6 %all_gather.48 = bf16[1,512,768]{1,2,0:T(8,128)(2,1)S(1)} all-gather(bf16[1,512,192]{1,2,0:T(8,128)(2,1)S(1)} %copy-done.70), channel_id=1, replica_groups=mesh['dp'=8,'tensor'=4] {'tensor'}, dimensions={2}, use_global_device_ids=true | all-gather | bytes 983040 | tf_op jit(solution)/shard_map/all_gather | solution.py:91
  63.3 6.8 all-gather.2
  70.1 5.3 fusion.171
  77.1 6.7 all-gather.4
  83.8 5.3 fusion.169
  89.1 13.1 %all_gather.54 = bf16[2,197,768]{1,2,0:T(8,128)(2,1)} all-gather(bf16[2,197,192]{1,2,0:T(8,128)(2,1)S(1)} %copy-done.72), channel_id=1, replica_groups=mesh['dp'=8,'tensor'=4] {'tensor'}, dimensions={2}, use_global_device_ids=true | all-gather | bytes 756480 | tf_op jit(solution)/shard_map/all_gather | solution.py:30
  104.3 7.5 all-reduce.8
  124.2 2.7 fusion.154
  129.6 3.6 multiply_convert_fusion.5
  133.1 2.9 convert_reduce_fusion.5
  136.9 2.8 convolution_convert_fusion.6
  139.7 3.0 copy.168
  142.7 2.8 copy.164
  163.2 10.4 %all_gather.56 = bf16[1,512,768]{1,2,0:T(8,128)(2,1)} all-gather(bf16[1,512,192]{1,2,0:T(8,128)(2,1)S(1)} %copy-done.71), channel_id=1, replica_groups=mesh['dp'=8,'tensor'=4] {'tensor'}, dimensions={2}, use_global_device_ids=true | all-gather | bytes 983040 | tf_op jit(solution)/shard_map/all_gather | solution.py:30
  173.7 51.0 %all-reduce.19.cloned.1.call-done = (bf16[1,512,768]{2,1,0:T(8,128)(2,1)}, bf16[1,711,768]{2,1,0:T(8,128)(2,1)}, bf16[2,197,768]{1,0,2:T(2,128)(2,1)}) async-done(((bf16[1,512,768]{2,1,0:T(8,128)(2,1)}, bf16[1,711,768]{2,1,0:T(8,128)(2,1)}, bf16[2,197,768]{1,0,2:T(2,128)(2,1)}), (bf16[1,512,768]{2,1,0:T(8,128)(2,1)}, bf16[1,711,768]{2,1,0:T(8,128)(2,1)}, ...) | async-done | bytes 2483728 | tf_op jit(solution)/shard_map/psum | solution.py:126
  224.7 2.9 fusion.133
  227.8 6.4 multiply_convert_fusion.3
  234.2 3.1 convert_reduce_fusion.4
  238.1 3.0 fusion.34
  241.1 4.8 copy.219
  248.5 3.2 fusion.33
  251.7 4.8 copy.215
  256.4 2.7 copy.264
  261.3 9.1 multiply_convert_fusion.2
  270.4 5.4 convert_reduce_fusion.2
  276.7 3.3 fusion.28
  280.1 6.7 copy.223
  286.8 2.9 copy.260
  300.5 2.9 convolution_convert_fusion.7
  303.4 3.1 copy.157
  310.1 3.6 fusion.27
  313.7 6.7 copy.217
  320.5 2.9 copy.261
  339.8 2.7 fusion.122
  343.0 12.4 %all-reduce.7 = (f32[2,197]{1,0:T(2,128)S(1)}, f32[2,197,1]{1,0,2:T(2,128)}, f32[512]{0:T(512)}, f32[1,512,1]{1,2,0:T(1,128)}, f32[711]{0:T(1024)}, /*index=5*/f32[1,711,1]{1,2,0:T(1,128)}) all-reduce(f32[2,197]{1,0:T(2,128)} %get-tuple-element.88, f32[2,197,1]{1,0,2:T(2,128)} %bitcast.536, ...), channel_id=1, replica_groups=mesh['dp'=8,'tensor'=4] {'tensor'}, use_global_device_ids=true, to_apply=%region_28.30 | all-reduce | flops 3234 | bytes 25872 | tf_op jit(solution)/shard_map/psum | solution.py:40
  356.1 3.0 convert_reduce_fusion.19
  360.8 8.9 all_gather.55
  376.4 2.7 fusion.30
  379.1 3.0 copy.178
  382.8 3.6 convert_reduce_fusion.17
  392.9 4.0 convert_reduce_fusion.11
  398.9 9.1 all_gather.57
  419.9 2.9 fusion.31
  422.8 3.5 copy.221
  429.5 3.2 convert_reduce_fusion.15
  432.8 5.3 multiply_reduce_fusion
  443.2 3.3 fusion.29
  446.5 5.8 copy.225
  458.4 2.9 copy.229
  461.3 2.8 reshape.1207
  470.1 3.3 pad_maximum_fusion.1
  473.4 11.1 %copy.231 = f32[3,768,768]{1,0,2:T(4,128)} copy(f32[3,768,768]{2,1,0:T(8,128)} %pad_maximum_fusion.1) | data formatting | bytes 14155776
  484.4 8.2 copy.246
  502.4 9.8 %copy.227 = f32[3,768,3,192]{3,2,0,1:T(4,128)} copy(f32[3,768,3,192]{1,3,2,0:T(8,128)} %pad_maximum_fusion.2) | data formatting | bytes 10616832
  512.2 11.2 %reshape.1205 = f32[768,1728]{1,0:T(8,128)} reshape(f32[768,3,3,192]{3,2,1,0:T(4,128)} %bitcast.442) | data formatting | bytes 10616832
  530.0 3.3 pad_maximum_fusion
  544.5 10.7 %all-reduce.6 = (f32[2,197]{1,0:T(2,128)S(1)}, f32[2,197,1]{1,0,2:T(2,128)S(1)}, f32[512]{0:T(512)S(1)}, f32[1,512,1]{1,2,0:T(1,128)S(1)}, f32[711]{0:T(1024)S(1)}, /*index=5*/f32[1,711,1]{1,2,0:T(1,128)S(1)}) all-reduce(f32[2,197]{1,0:T(2,128)S(1)} %get-tuple-element.106, ...), channel_id=1, replica_groups=mesh['dp'=8,'tensor'=4] {'tensor'}, use_global_device_ids=true, to_apply=%region_34.36 | all-reduce | flops 3234 | bytes 25872 | tf_op jit(solution)/shard_map/psum | solution.py:40
  564.2 38.5 %psum.127 = f32[3,12,192]{2,1,0:T(8,128)S(1)} all-reduce(f32[3,12,192]{2,1,0:T(8,128)S(1)} %pad_maximum_fusion.9), channel_id=1, replica_groups=mesh['dp'=8,'tensor'=4] {'dp'}, use_global_device_ids=true, to_apply=%region_85.87 | all-reduce | flops 6912 | bytes 55296 | tf_op jit(solution)/shard_map/psum | solution.py:344
  607.2 112.3 %reduce-scatter.47.cloned.1.call-done = f32[96,2304]{1,0:T(8,128)} async-done(((f32[768,2304]{1,0:T(8,128)}), f32[96,2304]{1,0:T(8,128)}) %reduce-scatter.47.cloned.1.call-update) | async-done | bytes 884752
  722.2 106.9 %reduce-scatter.43.cloned.1.call-done = f32[96,1728]{1,0:T(8,128)} async-done(((f32[768,1728]{1,0:T(8,128)}), f32[96,1728]{1,0:T(8,128)}) %reduce-scatter.43.cloned.1.call-update) | async-done | bytes 663568
  831.9 129.8 %reduce-scatter.29.cloned.1.call-done = f32[3,96,768]{2,1,0:T(8,128)} async-done(((f32[3,768,768]{2,1,0:T(8,128)}), f32[3,96,768]{2,1,0:T(8,128)}) %reduce-scatter.29.cloned.1.call-update) | async-done | bytes 884752 | tf_op jit(solution)/shard_map/reduce_scatter | solution.py:341
  (669 shorter events, 190.7 us)
Async XLA Ops:
  7.2 117.0 %all-reduce.15.cloned.1.call-start = ((), (), s32[]{:S(2)}) async-start(), calls=%async_computation.10 | async-start | bytes 1228800 | tf_op jit(solution)/shard_map/psum | solution.py:126
  8.5 104.7 %copy-start.140 = (bf16[2,192]{1,0:T(2,128)(2,1)}, bf16[2,192]{1,0:T(2,128)(2,1)S(1)}, u32[]{:S(2)}) copy-start(bf16[2,192]{1,0:T(2,128)(2,1)S(1)} %get-tuple-element.208) | copy-start | bytes 2308
  8.5 25.5 %collective-permute-start = (bf16[2,192]{1,0:T(2,128)(2,1)S(1)}, bf16[2,192]{1,0:T(2,128)(2,1)S(1)}, u32[]{:S(2)}, u32[]{:S(2)}) collective-permute-start(bf16[2,192]{1,0:T(2,128)(2,1)S(1)} %get-tuple-element.207), channel_id=1, source_target_pairs={{0,3},{1,0},{2,1},{3,2},{4,7},{5,4},{6,5},{7,6},{8,11},{9,8},{10,9... | collective-permute-start | bytes 2312 | tf_op jit(solution)/shard_map/ppermute | solution.py:85
  27.8 7.4 copy-start.135
  28.4 12.1 %copy-start.15 = (bf16[2,197,768]{2,1,0:T(8,128)(2,1)}, bf16[2,197,768]{2,1,0:T(8,128)(2,1)S(1)}, u32[]{:S(2)}) copy-start(bf16[2,197,768]{2,1,0:T(8,128)(2,1)S(1)} %copy.154) | copy-start | bytes 1815556
  28.7 11.8 %copy-start.109 = (f32[2,197]{1,0:T(2,128)}, f32[2,197]{1,0:T(2,128)S(1)}, u32[]{:S(2)}) copy-start(f32[2,197]{1,0:T(2,128)S(1)} %get-tuple-element.228) | copy-start | bytes 4732
  28.7 11.8 %copy-start.111 = (f32[2,197]{1,0:T(2,128)}, f32[2,197]{1,0:T(2,128)S(1)}, u32[]{:S(2)}) copy-start(f32[2,197]{1,0:T(2,128)S(1)} %get-tuple-element.229) | copy-start | bytes 4732
  34.1 3.6 collective-permute-start.1
  44.9 97.7 %all-gather.10.cloned.1.call-start = ((), (), s32[]{:S(2)}) async-start(), calls=%async_computation.11 | async-start | bytes 1474560 | tf_op jit(solution)/shard_map/all_gather | solution.py:91
  45.0 67.1 %collective-permute-start.2 = (bf16[2,192]{1,0:T(2,128)(2,1)S(1)}, bf16[2,192]{1,0:T(2,128)(2,1)S(1)}, u32[]{:S(2)}, u32[]{:S(2)}) collective-permute-start(bf16[2,192]{1,0:T(2,128)(2,1)S(1)} %get-tuple-element.209), channel_id=1, source_target_pairs={{0,3},{1,0},{2,1},{3,2},{4,7},{5,4},{6,5},{7,6},{8,11},{9,8},{10,9... | collective-permute-start | bytes 2312 | tf_op jit(solution)/shard_map/ppermute | solution.py:85
  45.1 68.2 %collective-permute-start.4 = (bf16[2,192]{1,0:T(2,128)(2,1)S(1)}, bf16[2,192]{1,0:T(2,128)(2,1)S(1)}, u32[]{:S(2)}, u32[]{:S(2)}) collective-permute-start(bf16[2,192]{1,0:T(2,128)(2,1)S(1)} %get-tuple-element.208), channel_id=1, source_target_pairs={{0,3},{1,0},{2,1},{3,2},{4,7},{5,4},{6,5},{7,6},{8,11},{9,8},{10,9... | collective-permute-start | bytes 2312 | tf_op jit(solution)/shard_map/ppermute | solution.py:85
  46.3 178.4 %all-reduce.19.cloned.1.call-start = ((), (), s32[]{:S(2)}) async-start(), calls=%async_computation.25 | async-start | bytes 5332992 | tf_op jit(solution)/shard_map/psum | solution.py:126
  50.3 68.2 %copy-start.133 = (pred[512]{0:T(512)(128)(4,1)}, pred[512]{0:T(512)(128)(4,1)S(1)}, u32[]{:S(2)}) copy-start(pred[512]{0:T(512)(128)(4,1)S(1)} %iota_compare_fusion.1) | copy-start | bytes 1540
  63.1 53.4 %copy-start.9 = (bf16[1,512,768]{2,1,0:T(8,128)(2,1)}, bf16[1,512,768]{2,1,0:T(8,128)(2,1)S(1)}, u32[]{:S(2)}) copy-start(bf16[1,512,768]{2,1,0:T(8,128)(2,1)S(1)} %copy.160) | copy-start | bytes 2359300
  70.1 19.1 %copy-start.72 = (bf16[2,197,192]{1,2,0:T(8,128)(2,1)S(1)}, bf16[2,197,192]{1,2,0:T(8,128)(2,1)}, u32[]{:S(2)}) copy-start(bf16[2,197,192]{1,2,0:T(8,128)(2,1)} %param.35) | copy-start | bytes 453892
  75.4 41.2 %copy-start.162 = (f32[768]{0:T(1024)}, f32[768]{0:T(1024)S(1)}, u32[]{:S(2)}) copy-start(f32[768]{0:T(1024)S(1)} %get-tuple-element.109) | copy-start | bytes 9220
  75.4 26.9 %copy-start.202 = (u32[32]{0:T(128)S(1)}, u32[32]{0:T(128)}, u32[]{:S(2)}) copy-start(u32[32]{0:T(128)} %constant.45) | copy-start | bytes 388
  75.4 36.4 %copy-start.192 = (f32[192]{0:T(256)S(1)}, f32[192]{0:T(256)}, u32[]{:S(2)}) copy-start(f32[192]{0:T(256)} %get-tuple-element.129) | copy-start | bytes 2308
  104.2 13.1 %copy-start.101 = (f32[512]{0:T(512)}, f32[512]{0:T(512)S(1)}, u32[]{:S(2)}) copy-start(f32[512]{0:T(512)S(1)} %get-tuple-element.224) | copy-start | bytes 6148
  104.2 13.1 %copy-start.103 = (f32[512]{0:T(512)}, f32[512]{0:T(512)S(1)}, u32[]{:S(2)}) copy-start(f32[512]{0:T(512)S(1)} %get-tuple-element.225) | copy-start | bytes 6148
  111.7 15.3 %copy-start.126 = (f32[768]{0:T(1024)}, f32[768]{0:T(1024)S(1)}, u32[]{:S(2)}) copy-start(f32[768]{0:T(1024)S(1)} %convert_element_type.878) | copy-start | bytes 9220
  111.9 8.6 copy-start.99
  112.0 38.1 %copy-start.120 = (f32[3,64]{1,0:T(4,128)}, f32[3,64]{1,0:T(4,128)S(1)}, u32[]{:S(2)}) copy-start(f32[3,64]{1,0:T(4,128)S(1)} %reshape.1120) | copy-start | bytes 2308
  112.1 44.3 %copy-start.122 = (f32[3,64]{1,0:T(4,128)}, f32[3,64]{1,0:T(4,128)S(1)}, u32[]{:S(2)}) copy-start(f32[3,64]{1,0:T(4,128)S(1)} %reshape.1119) | copy-start | bytes 2308
  112.1 3.6 collective-permute-start.3
  113.3 10.1 %collective-permute-start.5 = (bf16[2,384]{1,0:T(2,128)(2,1)S(1)}, bf16[2,384]{1,0:T(2,128)(2,1)S(1)}, u32[]{:S(2)}, u32[]{:S(2)}) collective-permute-start(bf16[2,384]{1,0:T(2,128)(2,1)S(1)} %pad_maximum_fusion.12), channel_id=1, source_target_pairs={{0,2},{1,3},{2,0},{3,1},{4,6},{5,7},{6,4},{7,5},{8,10},{9,11},{10,... | collective-permute-start | bytes 4616 | tf_op jit(solution)/shard_map/ppermute | solution.py:85
  124.2 23.0 %copy-start.190 = (f32[768]{0:T(1024)}, f32[768]{0:T(1024)S(1)}, u32[]{:S(2)}) copy-start(f32[768]{0:T(1024)S(1)} %get-tuple-element.134) | copy-start | bytes 9220
  161.3 109.0 %all-gather.12.cloned.1.call-start = ((), (), s32[]{:S(2)}) async-start(), calls=%async_computation.12 | async-start | bytes 1474560 | tf_op jit(solution)/shard_map/all_gather | solution.py:30
  161.9 163.9 %reduce-scatter.35.cloned.1.call-start = ((), (), s32[]{:S(2)}) async-start(), calls=%async_computation.17 | async-start | bytes 983040
  248.4 81.1 %reduce-scatter.31.cloned.1.call-start = ((), (), s32[]{:S(2)}) async-start(), calls=%async_computation.15 | async-start | bytes 983040
  248.5 12.8 %copy-start.130 = (f32[768]{0:T(1024)}, f32[768]{0:T(1024)S(1)}, u32[]{:S(2)}) copy-start(f32[768]{0:T(1024)S(1)} %convert_element_type.880) | copy-start | bytes 9220
  260.9 9.4 copy-start.87
  260.9 9.4 copy-start.89
  261.0 74.7 %reduce-scatter.39.cloned.1.call-start = ((), (), s32[]{:S(2)}) async-start(), calls=%async_computation.19 | async-start | bytes 1474560
  289.7 99.1 %reduce-scatter.33.cloned.1.call-start = ((), (), s32[]{:S(2)}) async-start(), calls=%async_computation.16 | async-start | bytes 1474560
  291.5 7.3 copy-start.147
  291.5 7.9 copy-start.153
  291.5 8.5 copy-start.148
  291.5 8.5 copy-start.149
  299.3 56.8 %copy-start.124 = (f32[1,192]{1,0:T(1,128)}, f32[1,192]{1,0:T(1,128)S(1)}, u32[]{:S(2)}) copy-start(f32[1,192]{1,0:T(1,128)S(1)} %get-tuple-element.218) | copy-start | bytes 2308
  323.4 104.3 %all-gather.14.cloned.1.call-start = ((), (), s32[]{:S(2)}) async-start(), calls=%async_computation.13 | async-start | bytes 1474560 | tf_op jit(solution)/shard_map/all_gather | solution.py:30
  323.4 9.7 %copy-start.114 = (f32[512]{0:T(512)S(1)}, f32[512]{0:T(512)}, u32[]{:S(2)}) copy-start(f32[512]{0:T(512)} %copy-done.113) | copy-start | bytes 6148
  323.5 9.7 %copy-start.117 = (f32[512]{0:T(512)S(1)}, f32[512]{0:T(512)}, u32[]{:S(2)}) copy-start(f32[512]{0:T(512)} %copy-done.116) | copy-start | bytes 6148
  355.4 15.8 %copy-start.150 = (f32[2,197]{1,0:T(2,128)}, f32[2,197]{1,0:T(2,128)S(1)}, u32[]{:S(2)}) copy-start(f32[2,197]{1,0:T(2,128)S(1)} %get-tuple-element.149) | copy-start | bytes 4732
  356.1 15.1 %copy-start.107 = (f32[2,197]{1,0:T(2,128)}, f32[2,197]{1,0:T(2,128)S(1)}, u32[]{:S(2)}) copy-start(f32[2,197]{1,0:T(2,128)S(1)} %multiply_bitcast_fusion.1) | copy-start | bytes 4732
  360.8 10.4 %copy-start.2 = (f32[2,3,197,197]{2,3,1,0:T(8,128)S(1)}, f32[2,3,197,197]{2,3,1,0:T(8,128)}, u32[]{:S(2)}) copy-start(f32[2,3,197,197]{2,3,1,0:T(8,128)} %copy-done.1) | copy-start | bytes 2794252
  360.8 10.4 %copy-start.30 = (f32[2,197,1,192]{1,3,2,0:T(8,128)S(1)}, f32[2,197,1,192]{1,3,2,0:T(8,128)}, u32[]{:S(2)}) copy-start(f32[2,197,1,192]{1,3,2,0:T(8,128)} %copy-done.29) | copy-start | bytes 907780
  398.8 137.5 %all-reduce.17.cloned.1.call-start = ((), (), s32[]{:S(2)}) async-start(), calls=%async_computation.24 | async-start | bytes 3145728
  398.9 11.3 %copy-start.5 = (bf16[3,512,512]{1,2,0:T(8,128)(2,1)S(1)}, bf16[3,512,512]{1,2,0:T(8,128)(2,1)}, u32[]{:S(2)}) copy-start(bf16[3,512,512]{1,2,0:T(8,128)(2,1)} %copy-done.4) | copy-start | bytes 4718596
  415.6 123.8 %reduce-scatter.37.cloned.1.call-start = ((), (), s32[]{:S(2)}) async-start(), calls=%async_computation.18 | async-start | bytes 983040
  427.5 114.3 %reduce-scatter.41.cloned.1.call-start = ((), (), s32[]{:S(2)}) async-start(), calls=%async_computation.20 | async-start | bytes 1474560
  429.5 8.6 slice-start
  432.8 9.7 %copy-start.53 = (bf16[3,64,711]{2,1,0:T(8,128)(2,1)}, bf16[3,64,711]{2,1,0:T(8,128)(2,1)S(1)}, u32[]{:S(2)}) copy-start(bf16[3,64,711]{2,1,0:T(8,128)(2,1)S(1)} %get-tuple-element.250) | copy-start | bytes 819076
  453.5 151.7 %reduce-scatter.45.cloned.1.call-start = ((), (), s32[]{:S(2)}) async-start(), calls=%async_computation.22 | async-start | bytes 2211840
  464.1 255.4 %reduce-scatter.47.cloned.1.call-start = ((), (), s32[]{:S(2)}) async-start(), calls=%async_computation.23 | async-start | bytes 7962624
  492.7 336.3 %reduce-scatter.43.cloned.1.call-start = ((), (), s32[]{:S(2)}) async-start(), calls=%async_computation.21 | async-start | bytes 6193152
  523.5 438.2 %reduce-scatter.29.cloned.1.call-start = ((), (), s32[]{:S(2)}) async-start(), calls=%async_computation.14 | async-start | bytes 7962624 | tf_op jit(solution)/shard_map/reduce_scatter | solution.py:341
  541.0 14.2 %copy-start.33 = (bf16[2,197,192]{2,1,0:T(8,128)(2,1)S(1)}, bf16[2,197,192]{2,1,0:T(8,128)(2,1)}, u32[]{:S(2)}) copy-start(bf16[2,197,192]{2,1,0:T(8,128)(2,1)} %copy.169) | copy-start | bytes 453892
  541.0 14.2 %copy-start.44 = (bf16[2,197,192]{2,1,0:T(8,128)(2,1)S(1)}, bf16[2,197,192]{2,1,0:T(8,128)(2,1)}, u32[]{:S(2)}) copy-start(bf16[2,197,192]{2,1,0:T(8,128)(2,1)} %copy.167) | copy-start | bytes 453892
  541.0 14.2 %copy-start.108 = (f32[2,197]{1,0:T(2,128)S(1)}, f32[2,197]{1,0:T(2,128)}, u32[]{:S(2)}) copy-start(f32[2,197]{1,0:T(2,128)} %copy-done.107) | copy-start | bytes 4732
  541.0 14.2 %copy-start.125 = (f32[1,192]{1,0:T(1,128)S(1)}, f32[1,192]{1,0:T(1,128)}, u32[]{:S(2)}) copy-start(f32[1,192]{1,0:T(1,128)} %copy-done.124) | copy-start | bytes 2308
  541.0 14.2 %copy-start.151 = (f32[2,197]{1,0:T(2,128)S(1)}, f32[2,197]{1,0:T(2,128)}, u32[]{:S(2)}) copy-start(f32[2,197]{1,0:T(2,128)} %copy-done.150) | copy-start | bytes 4732
  541.1 14.2 %copy-start.178 = (f32[1,192]{1,0:T(1,128)S(1)}, f32[1,192]{1,0:T(1,128)}, u32[]{:S(2)}) copy-start(f32[1,192]{1,0:T(1,128)} %get-tuple-element.220) | copy-start | bytes 2308
  543.9 17.6 %copy-start.43 = (f32[1,512,192]{2,1,0:T(8,128)S(1)}, f32[1,512,192]{2,1,0:T(8,128)}, u32[]{:S(2)}) copy-start(f32[1,512,192]{2,1,0:T(8,128)} %get-tuple-element.167) | copy-start | bytes 1179652
  (170 other events, 454.6 us)
Sparse Core Ops, SparseCore 0:
  45.1 36.9 all-reduce.14
  83.6 21.1 all-gather.9
  161.5 63.1 all-reduce.18
  226.1 17.4 all-gather.11
  248.5 23.3 reduce-scatter.34
  274.3 23.2 reduce-scatter.30
  300.1 25.5 reduce-scatter.38
  328.3 25.7 reduce-scatter.32
  398.9 17.5 all-gather.13
  419.9 42.8 all-reduce.16
  465.4 23.2 reduce-scatter.36
  491.1 25.6 reduce-scatter.40
  520.2 67.6 reduce-scatter.44
  591.4 128.0 reduce-scatter.46
  723.0 106.0 reduce-scatter.42
  833.2 128.5 reduce-scatter.28
